TPU v7x, 128 devices: a whole 4x4x4 slice. The times are simulated.
128 devices in a mesh: dp: 2 (over core), seq: 16 (over y, x), tensor: 4 (over z).
Axes of the slice: x: 4, y: 4, z: 4, core: 2. Of those that a mesh axis runs over, the one named last changes fastest.
Arguments:
- tokens: bfloat16 [2, 8192, 2048], P('dp', ('seq', 'tensor')), may hold values from -6 to 6
- attn_gain: float32 [2048], replicated, may hold values from 0.5 to 1.5
- w_qkv: bfloat16 [3, 2048, 2048], P(None, None, 'tensor'), may hold values from -1 to 1
- w_out: bfloat16 [2048, 2048], P('tensor'), may hold values from -0.125 to 0.125
- mlp_gain: float32 [2048], replicated, may hold values from 0.5 to 1.5
- w_up: bfloat16 [2048, 8192], P(None, 'tensor'), may hold values from -0.125 to 0.125
- w_down: bfloat16 [8192, 2048], P('tensor'), may hold values from -0.0625 to 0.0625
- pool_gain: float32 [2048], replicated, may hold values from -8 to 8
- pool_bias: float32 [2048], replicated, may hold values from 0.5 to 5
- value_weight: float32 [2048], replicated, may hold values from -6 to 6
- valid_frames: int32 [2], replicated, may hold values from 16 to 32, as said below
Outputs:
- hidden: bfloat16 [2, 8192, 2048], P('dp', ('seq', 'tensor'))
- frame_values: float32 [2, 32], P('dp', 'seq')
- advantages: float32 [2, 32], P('dp', 'seq')
Inputs may be any that keep to these rules, and one draw needn't show every extreme that they name: `valid_frames`: at least one rollout keeps all 32 frames and at least one keeps 32 // 2 of them.
All inputs are finite; a program needn't handle non-finite values.
Results may differ from a plain program's by a relative error of at most 0.017.
Values may be sent and summed in bfloat16 or wider, within the bound.
A program may use at most 256 MiB of HBM per device.

v0:
```python
import jax
import jax.numpy as jnp
from jax import lax
from jax.sharding import PartitionSpec as P

HEAD_DIM = 128
TOK_FRAME = 256
FR_DEV = 2


def laid_out(blocks, dim):
    shape = list(blocks.shape[1:])
    shape[dim] *= blocks.shape[0]
    return jnp.moveaxis(blocks, 0, dim).reshape(shape)


def sent_to_all(array, axis):
    copies = jnp.broadcast_to(array, (lax.axis_size(axis), *array.shape))
    return lax.all_to_all(copies, axis, split_axis=0, concat_axis=0, tiled=True)


def gathered_copies(array, axis, dim):
    return laid_out(sent_to_all(array, axis), dim)


def cut_along(array, dim, size):
    shape = array.shape
    blocks = array.reshape(*shape[:dim], size, shape[dim] // size, *shape[dim + 1 :])
    return jnp.moveaxis(blocks, dim, 0)


def summed_on_arrival(array, axis, dim):
    size = lax.axis_size(axis)
    blocks = lax.all_to_all(cut_along(array, dim, size), axis, 0, 0, tiled=True)
    return jnp.sum(blocks.astype(jnp.float32), axis=0)


def over_copies(array, axis):
    everything = sent_to_all(array, axis)
    return jnp.sum(everything, axis=0)


def collected_together(array, axis):
    leaves = jax.tree.leaves(array)
    sequence = sorted(range(len(leaves)), key=lambda k: -leaves[k].size)
    width = (1, *leaves[sequence[0]].shape)[-1]
    lines = [
        jnp.pad(leaves[k].reshape(-1), (0, -leaves[k].size % width)).reshape(-1, width)
        for k in sequence
    ]
    both, at, found = (sent_to_all(jnp.concatenate(lines), axis), 0, {})
    for k, line in zip(sequence, lines):
        piece = both[:, at : at + len(line)].reshape(len(both), -1)
        found[k] = piece[:, : leaves[k].size].reshape(-1, *leaves[k].shape)
        at += len(line)
    numbers = iter(range(len(leaves)))
    return jax.tree.map(lambda _: found[next(numbers)], array)


def combined_pairwise(pieces, combine):
    while len(jax.tree.leaves(pieces)[0]) > 1:
        pieces = jax.vmap(combine)(
            *(jax.tree.map(lambda part: part[side::2], pieces) for side in (0, 1))
        )
    return jax.tree.map(lambda part: part[0], pieces)


def entering_2(array, axis, combine, identity):
    size, index = (lax.axis_size(axis), lax.axis_index(axis))
    passed = jnp.arange(size) < index

    def kept(part, zero, own):
        part = jnp.where(
            passed.reshape(-1, *(1 for _ in own.shape)), part, jnp.asarray(zero, own.dtype)
        )
        return part

    pieces = collected_together(array, axis)
    return combined_pairwise(jax.tree.map(kept, pieces, identity, array), combine)


def rms_norm(values, gain):
    floats = values.astype(jnp.float32)
    square = jnp.mean(floats * floats, axis=-1, keepdims=True)
    return (floats * lax.rsqrt(square + 1e-05) * gain).astype(jnp.bfloat16)


def compose(earlier, later):
    return (earlier[0] * later[0], later[0] * earlier[1] + later[1])


def local(
    tokens,
    attn_gain,
    w_qkv,
    w_out,
    mlp_gain,
    w_up,
    w_down,
    pool_gain,
    pool_bias,
    value_weight,
    valid_frames,
):
    rows = tokens[0]
    row_count = rows.shape[0]
    seq_index = lax.axis_index("seq")
    tensor_index = lax.axis_index("tensor")
    roll_index = lax.axis_index("dp")
    length = valid_frames[roll_index]
    local_heads = w_qkv.shape[2] // HEAD_DIM
    scale = 1.0 / HEAD_DIM**0.5
    normed = rms_norm(rows, attn_gain)
    qkv = jnp.einsum(
        "nd,cde->nce",
        gathered_copies(normed, "tensor", 0),
        w_qkv,
        preferred_element_type=jnp.float32,
    ).astype(jnp.bfloat16)
    block = qkv.shape[0]
    query = qkv[:, 0].reshape(block, local_heads, HEAD_DIM)
    query_frame = (seq_index * block + jnp.arange(block, dtype=jnp.int32)) // TOK_FRAME
    peak = jnp.full((local_heads, block), -1e30, jnp.float32)
    key_piece = lax.all_gather(qkv[:, 1], "seq", axis=0, tiled=True)
    value_piece = lax.all_gather(qkv[:, 2], "seq", axis=0, tiled=True)
    width = key_piece.shape[0]
    key_heads = key_piece.reshape(width, local_heads, HEAD_DIM)
    value_heads = value_piece.reshape(width, local_heads, HEAD_DIM)
    scores = (
        jnp.einsum("qhe,khe->hqk", query, key_heads, preferred_element_type=jnp.float32) * scale
    )
    key_frame = jnp.arange(width, dtype=jnp.int32) // TOK_FRAME
    allowed = (key_frame[None, :] <= query_frame[:, None]) & (key_frame[None, :] < length)
    scores = jnp.where(allowed[None], scores, -1e30)
    new_peak = jnp.maximum(peak, jnp.max(scores, axis=-1))
    weights = jnp.where(allowed[None], jnp.exp(scores - new_peak[..., None]), 0.0)
    total = jnp.sum(weights, axis=-1)
    acc = jnp.einsum(
        "hqk,khe->hqe",
        weights.astype(jnp.bfloat16),
        value_heads,
        preferred_element_type=jnp.float32,
    )
    peak, total, acc = (new_peak, total, acc)
    mixed = (
        (acc / total[..., None])
        .transpose(1, 0, 2)
        .reshape(block, local_heads * HEAD_DIM)
        .astype(jnp.bfloat16)
    )
    attn_sum = summed_on_arrival(
        jnp.dot(mixed, w_out, preferred_element_type=jnp.float32).astype(jnp.bfloat16), "tensor", 0
    )
    after_attn = (rows.astype(jnp.float32) + attn_sum).astype(jnp.bfloat16)
    normed2 = rms_norm(after_attn, mlp_gain)
    up = jax.nn.gelu(
        jnp.dot(gathered_copies(normed2, "tensor", 0), w_up, preferred_element_type=jnp.float32),
        approximate=True,
    ).astype(jnp.bfloat16)
    down_sum = summed_on_arrival(
        jnp.dot(up, w_down, preferred_element_type=jnp.float32).astype(jnp.bfloat16), "tensor", 0
    )
    hidden = (after_attn.astype(jnp.float32) + down_sum).astype(jnp.bfloat16)
    local_frame = (tensor_index * row_count + jnp.arange(row_count, dtype=jnp.int32)) // TOK_FRAME
    selector = (local_frame[None, :] == jnp.arange(FR_DEV, dtype=jnp.int32)[:, None]).astype(
        jnp.bfloat16
    )
    sums = jnp.dot(selector, hidden, preferred_element_type=jnp.float32)
    sums = over_copies(sums, "tensor")
    gain, offset, head_weight = (pool_gain, pool_bias, value_weight)
    means = sums / TOK_FRAME
    frame_global = seq_index * FR_DEV + jnp.arange(FR_DEV, dtype=jnp.int32)
    valid = frame_global < length
    gate = jax.nn.sigmoid(means * gain + offset)
    decay = jnp.where(valid[:, None], gate, 1.0)
    source = jnp.where(valid[:, None], (1.0 - gate) * means, 0.0)
    agg_decay = jnp.ones_like(means[0])
    agg_source = jnp.zeros_like(means[0])
    for frame in range(FR_DEV):
        agg_decay, agg_source = compose((agg_decay, agg_source), (decay[frame], source[frame]))
    entering = entering_2(
        (agg_decay, agg_source),
        "seq",
        compose,
        (jnp.ones_like(agg_decay), jnp.zeros_like(agg_source)),
    )
    state = entering[1]
    collected = []
    for frame in range(FR_DEV):
        state = decay[frame] * state + source[frame]
        collected.append(jnp.sum(state * head_weight))
    partial_values = jnp.stack(collected)
    values = jnp.where(valid, partial_values, 0.0)
    pick = jnp.sum(jnp.where(frame_global == length - 1, values, 0.0))
    count = jnp.sum(valid_frames).astype(jnp.float32)
    slot = (jnp.arange(lax.axis_size("dp"), dtype=jnp.int32) == roll_index).astype(jnp.float32)
    entries = jnp.stack([pick, jnp.sum(values), jnp.sum(values * values)])
    table = over_copies(entries[:, None] * slot[None, :], ("dp", "seq"))
    finals, first_sums, second_sums = (table[0], table[1], table[2])
    lengths = valid_frames.astype(jnp.float32)
    mean = jnp.sum(lengths * finals - first_sums) / count
    squares = jnp.sum(lengths * finals * finals - 2.0 * finals * first_sums + second_sums) / count
    variance = squares - mean * mean
    final = jnp.sum(finals * slot)
    gap = jnp.where(valid, final - values, 0.0)
    centered = jnp.where(valid, gap - mean, 0.0)
    advantages = jnp.where(valid, centered * lax.rsqrt(variance + 1e-05), 0.0)
    return (hidden[None], values[None], advantages[None])


def solution(mesh):
    in_specs = (
        P("dp", ("seq", "tensor"), None),
        P(),
        P(None, None, "tensor"),
        P("tensor", None),
        P(),
        P(None, "tensor"),
        P("tensor", None),
        P(),
        P(),
        P(),
        P(),
    )
    out_specs = (P("dp", ("seq", "tensor"), None), P("dp", "seq"), P("dp", "seq"))
    return jax.shard_map(local, mesh=mesh, in_specs=in_specs, out_specs=out_specs, check_vma=False)
```

profile of v0, /device:TPU:1, one launch (start us, length us, event | category | flops | bytes accessed | tf_op | source)
XLA Modules:
  0.0 397.9 jit_solution(1395034552048912833)
XLA Ops:
  7.2 1.4 fusion.25
  8.6 1.7 fusion.27
  10.3 0.2 broadcast_in_dim.104
  10.6 31.1 %all_to_all.35 = bf16[4,128,2048]{2,1,0:T(8,128)(2,1)S(1)} all-to-all(bf16[4,128,2048]{2,1,0:T(8,128)(2,1)S(1)} %broadcast_in_dim.104), channel_id=1, replica_groups=mesh['dp'=2,'seq'=16,'tensor'=4] {'tensor'}, dimensions={0} | all-to-all | bytes 4194304 | tf_op jit(solution)/shard_map/all_to_all | solution.py:19
  41.7 3.5 convolution_convert_fusion.2
  45.2 1.1 fusion.63
  46.3 0.7 all-gather.7.cloned.1.call-update
  47.0 0.6 dynamic_slice.3
  47.6 0.6 broadcast_compare_fusion
  48.3 4.9 %compare_and_fusion = pred[512,8192]{1,0:T(8,128)(4,1)} fusion(s32[8192]{0:T(1024)S(1)} %add_select_fusion, s32[512]{0:T(512)S(1)} %add_select_fusion.1, pred[8192]{0:T(1024)(128)(4,1)S(1)} %broadcast_compare_fusion), kind=kLoop, calls=%fused_computation.7 | loop fusion | flops 8388608 | bytes 4237312 | tf_op jit(solution)/shard_map/and | solution.py:133
  53.2 69.6 %all-gather.5.cloned.1.call-done = bf16[8192,1,512]{0,2,1:T(8,128)(2,1)} async-done(((bf16[512,1,512]{0,2,1:T(8,128)(2,1)}), bf16[8192,1,512]{0,2,1:T(8,128)(2,1)}) %all-gather.5.cloned.1.call-update) | async-done | bytes 8388624 | tf_op jit(solution)/shard_map/all_gather | solution.py:124
  122.8 30.0 %fusion = (f32[4,512]{1,0:T(4,128)S(1)}, f32[4,512,8192]{2,1,0:T(8,128)}) fusion(pred[512,8192]{1,0:T(8,128)(4,1)} %compare_and_fusion, bf16[512,4,128]{0,2,1:T(8,128)(2,1)S(1)} %bitcast.73, bf16[8192,4,128]{0,2,1:T(8,128)(2,1)} %bitcast.78), kind=kOutput, calls=%fused_computation.2 | convolution fusion | flops 4345296896 | bytes 80224256 | tf_op jit(solution)/shard_map/qhe,khe->hqk/dot_general | solution.py:130
  152.8 23.6 %fusion.1 = f32[4,512]{1,0:T(4,128)S(1)} fusion(f32[4,512,8192]{2,1,0:T(8,128)} %get-tuple-element.36, f32[4,512]{1,0:T(4,128)S(1)} %broadcast_maximum_fusion, pred[512,8192]{1,0:T(8,128)(4,1)} %compare_and_fusion), kind=kLoop, calls=%fused_computation.3 | loop fusion | flops 83884032 | bytes 71319552 | tf_op jit(solution)/shard_map/reduce_sum | solution.py:137
  176.4 25.0 %all-gather.7.cloned.1.call-done = bf16[8192,1,512]{0,2,1:T(8,128)(2,1)} async-done(((bf16[512,1,512]{0,2,1:T(8,128)(2,1)}), bf16[8192,1,512]{0,2,1:T(8,128)(2,1)}) %all-gather.7.cloned.1.call-update) | async-done | bytes 8388624 | tf_op jit(solution)/shard_map/all_gather | solution.py:125
  201.4 28.9 %divide_convert_fusion = bf16[512,4,128]{0,2,1:T(8,128)(2,1)S(1)} fusion(bf16[8192,4,128]{0,2,1:T(8,128)(2,1)} %bitcast.79, f32[4,512,8192]{2,1,0:T(8,128)} %get-tuple-element.36, f32[4,512]{1,0:T(4,128)S(1)} %broadcast_maximum_fusion, pred[512,8192]{1,0:T(8,128)(4,1)} %compare_and_fusion, f32[512,4]{0,1:T(4,128)S(1)} %bitcast.77), kind=kOutput, calls=%fused_computation.46 | convolution fusion | flops 4379377664 | bytes 80232448 | tf_op jit(solution)/shard_map/hqk,khe->hqe/dot_general | solution.py:138
  230.4 1.3 convolution_convert_fusion.1
  231.7 28.0 %all_to_all.36 = bf16[4,128,2048]{2,1,0:T(8,128)(2,1)S(1)} all-to-all(bf16[4,128,2048]{2,1,0:T(8,128)(2,1)S(1)} %bitcast.71), channel_id=1, replica_groups=mesh['dp'=2,'seq'=16,'tensor'=4] {'tensor'}, dimensions={0} | all-to-all | bytes 4194304 | tf_op jit(solution)/shard_map/all_to_all | solution.py:34
  259.7 0.4 convert_reduce_fusion.1
  260.1 0.3 fusion.30
  260.3 0.8 copy-done.3
  261.6 26.4 %all_to_all.37 = bf16[4,128,2048]{2,1,0:T(8,128)(2,1)} all-to-all(bf16[4,128,2048]{2,1,0:T(8,128)(2,1)S(1)} %broadcast_in_dim.108), channel_id=1, replica_groups=mesh['dp'=2,'seq'=16,'tensor'=4] {'tensor'}, dimensions={0} | all-to-all | bytes 4194304 | tf_op jit(solution)/shard_map/all_to_all | solution.py:19
  288.0 16.6 %convolution_convert_fusion = bf16[512,2048]{1,0:T(8,128)(2,1)} fusion(bf16[2048,2048]{1,0:T(8,128)(2,1)} %param.17, bf16[512,2048]{1,0:T(8,128)(2,1)} %bitcast.72, bf16[2048,2048]{1,0:T(8,128)(2,1)} %param.16), kind=kOutput, calls=%fused_computation.19 | convolution fusion | flops 8600420352 | bytes 20971520 | tf_op jit(solution)/shard_map/dot_general | solution.py:161
  304.6 4.6 %all-to-all-start.3 = ((bf16[4,128,2048]{2,1,0:T(8,128)(2,1)}), bf16[4,128,2048]{2,1,0:T(8,128)(2,1)}, u32[]{:S(2)}, u32[]{:S(2)}) async-start(bf16[4,128,2048]{2,1,0:T(8,128)(2,1)} %bitcast.69), calls=%async_computation.3 | async-start | bytes 4194304 | tf_op jit(solution)/shard_map/all_to_all | solution.py:34
  309.2 22.3 %all-to-all-done.3 = bf16[4,128,2048]{2,1,0:T(8,128)(2,1)} async-done(((bf16[4,128,2048]{2,1,0:T(8,128)(2,1)}), bf16[4,128,2048]{2,1,0:T(8,128)(2,1)}, u32[]{:S(2)}, u32[]{:S(2)}) %all-to-all-start.3) | async-done | bytes 2097184 | tf_op jit(solution)/shard_map/all_to_all | solution.py:34
  331.5 2.1 convert_reduce_fusion
  333.7 1.0 copy-done.1
  334.6 1.3 fusion.37
  335.9 0.6 broadcast_in_dim.110
  336.6 3.3 all-to-all-start.4
  339.9 0.6 fusion.54
  340.5 3.8 all-to-all-done.4
  344.5 0.6 fusion.67
  345.1 0.8 broadcast_in_dim.113
  345.9 4.7 %all-to-all-start.5 = ((f32[16,2,2048]{2,1,0:T(2,128)}), f32[16,2,2048]{2,1,0:T(2,128)S(1)}, u32[]{:S(2)}, u32[]{:S(2)}) async-start(f32[16,2,2048]{2,1,0:T(2,128)} %broadcast_in_dim.113), calls=%async_computation.5 | async-start | bytes 524288 | tf_op jit(solution)/shard_map/all_to_all | solution.py:19
  350.6 0.6 reduce_sum.164
  352.5 0.6 compare_convert_fusion
  353.1 5.0 %all-to-all-done.5 = f32[16,2,2048]{2,1,0:T(2,128)S(1)} async-done(((f32[16,2,2048]{2,1,0:T(2,128)}), f32[16,2,2048]{2,1,0:T(2,128)S(1)}, u32[]{:S(2)}, u32[]{:S(2)}) %all-to-all-start.5) | async-done | bytes 262176 | tf_op jit(solution)/shard_map/all_to_all | solution.py:19
  358.9 0.8 fusion.45
  359.7 1.4 multiply_reduce_fusion.1
  361.1 2.5 fusion.52
  363.6 2.0 pad_maximum_fusion.1
  365.6 0.7 broadcast_multiply_fusion.1
  366.3 0.6 broadcast_in_dim.118
  366.9 11.1 %all-to-all-start.6 = ((f32[32,3,2]{1,2,0:T(2,128)}), f32[32,3,2]{1,2,0:T(2,128)S(1)}, u32[]{:S(2)}, u32[]{:S(2)}) async-start(f32[32,3,2]{1,2,0:T(2,128)} %broadcast_in_dim.118), calls=%async_computation.6 | async-start | bytes 65536 | tf_op jit(solution)/shard_map/all_to_all | solution.py:19
  378.1 2.3 fusion.34
  380.4 4.7 %all-to-all-done.6 = f32[32,3,2]{1,2,0:T(2,128)S(1)} async-done(((f32[32,3,2]{1,2,0:T(2,128)}), f32[32,3,2]{1,2,0:T(2,128)S(1)}, u32[]{:S(2)}, u32[]{:S(2)}) %all-to-all-start.6) | async-done | bytes 800 | tf_op jit(solution)/shard_map/all_to_all | solution.py:19
  385.3 1.4 subtract_reduce_fusion
  388.0 3.1 multiply_select_fusion.2
  (54 shorter events, 1.8 us)
Async XLA Ops:
  7.2 223.2 %copy-start = (bf16[512,2048]{1,0:T(8,128)(2,1)S(1)}, bf16[512,2048]{1,0:T(8,128)(2,1)}, u32[]{:S(2)}) copy-start(bf16[512,2048]{1,0:T(8,128)(2,1)} %param.14) | copy-start | bytes 6291460
  7.2 115.6 %all-gather.5.cloned.1.call-start = ((), (), s32[]{:S(2)}) async-start(), calls=%async_computation.7 | async-start | bytes 8912896 | tf_op jit(solution)/shard_map/all_gather | solution.py:124
  7.2 34.5 %copy-start.9 = (bf16[3,2048,512]{2,1,0:T(8,128)(2,1)S(1)}, bf16[3,2048,512]{2,1,0:T(8,128)(2,1)}, u32[]{:S(2)}) copy-start(bf16[3,2048,512]{2,1,0:T(8,128)(2,1)} %param.13) | copy-start | bytes 18874372
  41.7 5.3 %copy-start.8 = (s32[2]{0:T(128)S(1)}, s32[2]{0:T(128)}, u32[]{:S(2)}) copy-start(s32[2]{0:T(128)} %param.21) | copy-start | bytes 28
  46.3 155.1 %all-gather.7.cloned.1.call-start = ((), (), s32[]{:S(2)}) async-start(), calls=%async_computation.8 | async-start | bytes 8912896 | tf_op jit(solution)/shard_map/all_gather | solution.py:125
  230.4 29.7 %copy-start.2 = (bf16[1,128,2048]{2,1,0:T(8,128)(2,1)S(1)}, bf16[1,128,2048]{2,1,0:T(8,128)(2,1)}, u32[]{:S(2)}) copy-start(bf16[1,128,2048]{2,1,0:T(8,128)(2,1)} %param.11) | copy-start | bytes 1572868
  230.4 30.7 %copy-start.5 = (f32[2048]{0:T(1024)S(1)}, f32[2048]{0:T(1024)}, u32[]{:S(2)}) copy-start(f32[2048]{0:T(1024)} %param.15) | copy-start | bytes 24580
  260.3 0.8 copy-start.3
  288.0 21.2 %copy-start.6 = (f32[2048]{0:T(1024)S(1)}, f32[2048]{0:T(1024)}, u32[]{:S(2)}) copy-start(f32[2048]{0:T(1024)} %param.18) | copy-start | bytes 24580
  304.6 39.8 %copy-start.7 = (f32[2048]{0:T(1024)S(1)}, f32[2048]{0:T(1024)}, u32[]{:S(2)}) copy-start(f32[2048]{0:T(1024)} %param.19) | copy-start | bytes 24580
  304.6 27.0 %all-to-all-start.3 = ((bf16[4,128,2048]{2,1,0:T(8,128)(2,1)}), bf16[4,128,2048]{2,1,0:T(8,128)(2,1)}, u32[]{:S(2)}, u32[]{:S(2)}) async-start(bf16[4,128,2048]{2,1,0:T(8,128)(2,1)} %bitcast.69), calls=%async_computation.3 | async-start | bytes 4194304 | tf_op jit(solution)/shard_map/all_to_all | solution.py:34
  333.7 1.0 copy-start.1
  336.6 7.7 %all-to-all-start.4 = ((f32[4,2,2048]{2,1,0:T(2,128)}), f32[4,2,2048]{2,1,0:T(2,128)S(1)}, u32[]{:S(2)}, u32[]{:S(2)}) async-start(f32[4,2,2048]{2,1,0:T(2,128)} %broadcast_in_dim.110), calls=%async_computation.4 | async-start | bytes 131072 | tf_op jit(solution)/shard_map/all_to_all | solution.py:19
  344.4 1.5 copy-start.4
  345.9 12.2 %all-to-all-start.5 = ((f32[16,2,2048]{2,1,0:T(2,128)}), f32[16,2,2048]{2,1,0:T(2,128)S(1)}, u32[]{:S(2)}, u32[]{:S(2)}) async-start(f32[16,2,2048]{2,1,0:T(2,128)} %broadcast_in_dim.113), calls=%async_computation.5 | async-start | bytes 524288 | tf_op jit(solution)/shard_map/all_to_all | solution.py:19
  366.9 18.1 %all-to-all-start.6 = ((f32[32,3,2]{1,2,0:T(2,128)}), f32[32,3,2]{1,2,0:T(2,128)S(1)}, u32[]{:S(2)}, u32[]{:S(2)}) async-start(f32[32,3,2]{1,2,0:T(2,128)} %broadcast_in_dim.118), calls=%async_computation.6 | async-start | bytes 65536 | tf_op jit(solution)/shard_map/all_to_all | solution.py:19
Sparse Core Ops, SparseCore 0:
  46.4 76.3 all-gather.4
  124.9 76.4 all-gather.6
where the time goes:
time: 399 us; the launch traced here: 398 us
  waiting for transfers between devices  131 us (33%)
  blocking collectives  85.5 us (21%)
  matrix products  81.5 us (20%)
  other arithmetic  52.2 us (13%)
  starting transfers between devices  23.7 us (6%)
  between operations  17 us (4%)
  local copies, waits for them, and re-layouts  6.76 us (2%)
    all_gather x1, waiting for transfers between devices, local(): key_piece = lax.all_gather(qkv[:, 1], 'seq', axis=0, tiled=True)  69.6 us
    all_to_all x2, blocking collectives, sent_to_all(): return lax.all_to_all(copies, axis, split_axis=0, concat_axis=0, tiled=True)  57.6 us
    dot_general x1, matrix products, local(): jnp.einsum('qhe,khe->hqk', query, key_heads, preferred_element_type=jnp.f...  30 us
    dot_general x1, matrix products, local(): jnp.einsum('hqk,khe->hqe', weights.astype(jnp.bfloat16), value_heads, pre...  28.9 us
    all_to_all x1, blocking collectives, summed_on_arrival(): blocks = lax.all_to_all(cut_along(array, dim, size), axis, 0, 0, tiled=True)  28 us
    all_gather x1, waiting for transfers between devices, local(): value_piece = lax.all_gather(qkv[:, 2], 'seq', axis=0, tiled=True)  25 us
    reduce_sum x1, other arithmetic, local(): total = jnp.sum(weights, axis=-1)  23.6 us
    all_to_all x1, waiting for transfers between devices, summed_on_arrival(): blocks = lax.all_to_all(cut_along(array, dim, size), axis, 0, 0, tiled=True)  22.3 us
  transfers between devices with their start and end apart: 6, of which 6 were waited for; matrix products, arithmetic and copies ran while one was open for 16% of the time, Pallas kernels for 0%

commit v1 on v0

--- a/solution.py
+++ b/solution.py
@@ -102,6 +102,19 @@
     value_weight,
     valid_frames,
 ):
+
+    def update_space(sample):
+        many = lax.psum(1, "seq")
+        inbox = [(q, (q + 1) % many) for q in range(many)]
+        by_rank = [(q, (q - 1) % many) for q in range(many)]
+        step_out, inter = ([sample], [sample])
+        for _ in range(many // 2):
+            step_out.append(lax.ppermute(step_out[-1], "seq", inbox))
+        for _ in range((many - 1) // 2):
+            inter.append(lax.ppermute(inter[-1], "seq", by_rank))
+        val2 = jnp.concatenate([*step_out[::-1], *inter[1:]], axis=0)
+        return jnp.roll(val2, (lax.axis_index("seq") - many // 2) * sample.shape[0], axis=0)
+
     rows = tokens[0]
     row_count = rows.shape[0]
     seq_index = lax.axis_index("seq")
@@ -122,7 +135,7 @@
     query_frame = (seq_index * block + jnp.arange(block, dtype=jnp.int32)) // TOK_FRAME
     peak = jnp.full((local_heads, block), -1e30, jnp.float32)
     key_piece = lax.all_gather(qkv[:, 1], "seq", axis=0, tiled=True)
-    value_piece = lax.all_gather(qkv[:, 2], "seq", axis=0, tiled=True)
+    value_piece = update_space(qkv[:, 2])
     width = key_piece.shape[0]
     key_heads = key_piece.reshape(width, local_heads, HEAD_DIM)
     value_heads = value_piece.reshape(width, local_heads, HEAD_DIM)

time: 399 us -> 495 us (1.24); the launches traced: 398 us -> 486 us
  local copies, waits for them, and re-layouts: 6.76 us -> 63.7 us
  starting transfers between devices: 23.7 us -> 77.1 us
  waiting for transfers between devices: 131 us -> 113 us
  blocking collectives: 85.5 us -> 79.2 us
    ppermute x0 -> x15, waiting for transfers between devices: none -> 82.7 us  [the longest x8 67.8 us: update_space(): step_out.append(lax.ppermute(step_out[-1], 'seq', inbox))]
    all_gather x1, waiting for transfers between devices: 69.6 us -> 0.01 us  [local(): key_piece = lax.all_gather(qkv[:, 1], 'seq', axis=0, tiled=True)]
    ppermute x0 -> x15, starting transfers between devices: none -> 49.6 us  [the longest x7 36.9 us: update_space(): inter.append(lax.ppermute(inter[-1], 'seq', by_rank))]
    unnamed x20 -> x77, local copies, waits for them, and re-layouts: 1.8 us -> 50.1 us
    all_gather x1 -> x0, waiting for transfers between devices: 25 us -> none  [local(): value_piece = lax.all_gather(qkv[:, 2], 'seq', axis=0, tiled=True)]
    dynamic_slice x0 -> x1, local copies, waits for them, and re-layouts: none -> 7.68 us  [update_space(): jnp.roll(val2, (lax.axis_index('seq') - many // 2) * sample.shape[0], axi...]
    all_to_all x1, waiting for transfers between devices: 22.3 us -> 17 us  [summed_on_arrival(): blocks = lax.all_to_all(cut_along(array, dim, size), axis, 0, 0, tiled=True)]
    all_to_all x2, blocking collectives: 57.6 us -> 52.5 us  [sent_to_all(): return lax.all_to_all(copies, axis, split_axis=0, concat_axis=0, tiled=True)]
  transfers between devices with their start and end apart: 6 -> 20, of which waited for: 6 -> 17; matrix products, arithmetic and copies ran while one was open for 16% -> 14% of each run, Pallas kernels for 0% -> 0%
where the time goes in v1:
time: 495 us; the launch traced here: 486 us
  waiting for transfers between devices  113 us (23%)
  matrix products  83.4 us (17%)
  blocking collectives  79.2 us (16%)
  starting transfers between devices  77.1 us (16%)
  local copies, waits for them, and re-layouts  63.7 us (13%)
  other arithmetic  52 us (11%)
  between operations  17.4 us (4%)
    ppermute x8, waiting for transfers between devices, update_space(): step_out.append(lax.ppermute(step_out[-1], 'seq', inbox))  67.8 us
    all_to_all x2, blocking collectives, sent_to_all(): return lax.all_to_all(copies, axis, split_axis=0, concat_axis=0, tiled=True)  52.5 us
    unnamed x77, local copies, waits for them, and re-layouts  50.1 us
    ppermute x7, starting transfers between devices, update_space(): inter.append(lax.ppermute(inter[-1], 'seq', by_rank))  36.9 us
    dot_general x1, matrix products, local(): jnp.einsum('qhe,khe->hqk', query, key_heads, preferred_element_type=jnp.f...  29 us
    dot_general x1, matrix products, local(): jnp.einsum('hqk,khe->hqe', weights.astype(jnp.bfloat16), value_heads, pre...  29 us
    all_to_all x1, blocking collectives, summed_on_arrival(): blocks = lax.all_to_all(cut_along(array, dim, size), axis, 0, 0, tiled=True)  26.7 us
    all_to_all x3, starting transfers between devices, sent_to_all(): return lax.all_to_all(copies, axis, split_axis=0, concat_axis=0, tiled=True)  23 us
  transfers between devices with their start and end apart: 20, of which 17 were waited for; matrix products, arithmetic and copies ran while one was open for 14% of the time, Pallas kernels for 0%

profile of v1, /device:TPU:1, one launch (start us, length us, event | category | flops | bytes accessed | tf_op | source)
XLA Modules:
  0.0 486.0 jit_solution(5691042466854007468)
XLA Ops:
  10.1 31.1 %all_to_all.35 = bf16[4,128,2048]{2,1,0:T(8,128)(2,1)S(1)} all-to-all(bf16[4,128,2048]{2,1,0:T(8,128)(2,1)S(1)} %broadcast_in_dim.104), channel_id=1, replica_groups=mesh['dp'=2,'seq'=16,'tensor'=4] {'tensor'}, dimensions={0} | all-to-all | bytes 4194304 | tf_op jit(solution)/shard_map/all_to_all | solution.py:19
  41.2 6.3 %convolution_convert_fusion.2 = bf16[512,3,512]{0,2,1:T(8,128)(2,1)S(1)} fusion(bf16[512,2048,1]{1,0,2:T(8,128)(2,1)S(1)} %bitcast.77, bf16[3,2048,512]{2,1,0:T(8,128)(2,1)} %param.13), kind=kOutput, calls=%fused_computation.25 | convolution fusion | flops 3222011904 | bytes 9961472 | tf_op jit(solution)/shard_map/nd,cde->nce/dot_general | solution.py:127
  51.1 14.1 %collective-permute-done = bf16[512,512]{0,1:T(8,128)(2,1)S(1)} collective-permute-done((bf16[512,512]{0,1:T(8,128)(2,1)S(1)}, bf16[512,512]{0,1:T(8,128)(2,1)S(1)}, u32[]{:S(2)}, u32[]{:S(2)}) %collective-permute-start) | collective-permute-done | bytes 524320 | tf_op jit(solution)/shard_map/ppermute | solution.py:112
  65.2 4.8 collective-permute-start.8
  70.0 13.6 %collective-permute-done.1 = bf16[512,512]{0,1:T(8,128)(2,1)S(1)} collective-permute-done((bf16[512,512]{0,1:T(8,128)(2,1)S(1)}, bf16[512,512]{0,1:T(8,128)(2,1)S(1)}, u32[]{:S(2)}, u32[]{:S(2)}) %collective-permute-start.1) | collective-permute-done | bytes 524320 | tf_op jit(solution)/shard_map/ppermute | solution.py:112
  84.4 5.4 %collective-permute-start.9 = (bf16[512,512]{0,1:T(8,128)(2,1)S(1)}, bf16[512,512]{0,1:T(8,128)(2,1)S(1)}, u32[]{:S(2)}, u32[]{:S(2)}) collective-permute-start(bf16[512,512]{0,1:T(8,128)(2,1)S(1)} %collective-permute-done.8), channel_id=1, source_target_pairs={{0,60},{4,0},{8,4},{12,8},{16,12},{20,16},{24,20},{28,24},{32,28},... | collective-permute-start | bytes 1572872 | tf_op jit(solution)/shard_map/ppermute | solution.py:114
  89.8 5.6 %collective-permute-done.2 = bf16[512,512]{0,1:T(8,128)(2,1)S(1)} collective-permute-done((bf16[512,512]{0,1:T(8,128)(2,1)S(1)}, bf16[512,512]{0,1:T(8,128)(2,1)S(1)}, u32[]{:S(2)}, u32[]{:S(2)}) %collective-permute-start.2) | collective-permute-done | bytes 524320 | tf_op jit(solution)/shard_map/ppermute | solution.py:112
  95.4 2.0 collective-permute-done.9
  97.4 5.5 %collective-permute-start.10 = (bf16[512,512]{0,1:T(8,128)(2,1)S(1)}, bf16[512,512]{0,1:T(8,128)(2,1)S(1)}, u32[]{:S(2)}, u32[]{:S(2)}) collective-permute-start(bf16[512,512]{0,1:T(8,128)(2,1)S(1)} %collective-permute-done.9), channel_id=1, source_target_pairs={{0,60},{4,0},{8,4},{12,8},{16,12},{20,16},{24,20},{28,24},{32,28},... | collective-permute-start | bytes 1572872 | tf_op jit(solution)/shard_map/ppermute | solution.py:114
  102.9 3.8 collective-permute-done.3
  106.8 2.9 collective-permute-done.10
  109.6 5.5 %collective-permute-start.11 = (bf16[512,512]{0,1:T(8,128)(2,1)S(1)}, bf16[512,512]{0,1:T(8,128)(2,1)}, u32[]{:S(2)}, u32[]{:S(2)}) collective-permute-start(bf16[512,512]{0,1:T(8,128)(2,1)S(1)} %collective-permute-done.10), channel_id=1, source_target_pairs={{0,60},{4,0},{8,4},{12,8},{16,12},{20,16},{24,20},{28,24},{32,28},... | collective-permute-start | bytes 1572872 | tf_op jit(solution)/shard_map/ppermute | solution.py:114
  115.1 3.5 collective-permute-done.4
  118.6 2.6 collective-permute-done.11
  121.3 5.3 %collective-permute-start.12 = (bf16[512,512]{0,1:T(8,128)(2,1)}, bf16[512,512]{0,1:T(8,128)(2,1)}, u32[]{:S(2)}, u32[]{:S(2)}) collective-permute-start(bf16[512,512]{0,1:T(8,128)(2,1)} %collective-permute-done.11), channel_id=1, source_target_pairs={{0,60},{4,0},{8,4},{12,8},{16,12},{20,16},{24,20},{28,24},{32,28},... | collective-permute-start | bytes 1572872 | tf_op jit(solution)/shard_map/ppermute | solution.py:114
  126.6 5.1 %collective-permute-done.5 = bf16[512,512]{0,1:T(8,128)(2,1)} collective-permute-done((bf16[512,512]{0,1:T(8,128)(2,1)S(1)}, bf16[512,512]{0,1:T(8,128)(2,1)}, u32[]{:S(2)}, u32[]{:S(2)}) %collective-permute-start.5) | collective-permute-done | bytes 524320 | tf_op jit(solution)/shard_map/ppermute | solution.py:112
  133.0 6.6 %collective-permute-done.12 = bf16[512,512]{0,1:T(8,128)(2,1)} collective-permute-done((bf16[512,512]{0,1:T(8,128)(2,1)}, bf16[512,512]{0,1:T(8,128)(2,1)}, u32[]{:S(2)}, u32[]{:S(2)}) %collective-permute-start.12) | collective-permute-done | bytes 524320 | tf_op jit(solution)/shard_map/ppermute | solution.py:114
  139.6 5.5 %collective-permute-start.13 = (bf16[512,512]{0,1:T(8,128)(2,1)}, bf16[512,512]{0,1:T(8,128)(2,1)}, u32[]{:S(2)}, u32[]{:S(2)}) collective-permute-start(bf16[512,512]{0,1:T(8,128)(2,1)} %collective-permute-done.12), channel_id=1, source_target_pairs={{0,60},{4,0},{8,4},{12,8},{16,12},{20,16},{24,20},{28,24},{32,28},... | collective-permute-start | bytes 1572872 | tf_op jit(solution)/shard_map/ppermute | solution.py:114
  145.1 12.8 %collective-permute-done.6 = bf16[512,512]{0,1:T(8,128)(2,1)} collective-permute-done((bf16[512,512]{0,1:T(8,128)(2,1)}, bf16[512,512]{0,1:T(8,128)(2,1)}, u32[]{:S(2)}, u32[]{:S(2)}) %collective-permute-start.6) | collective-permute-done | bytes 524320 | tf_op jit(solution)/shard_map/ppermute | solution.py:112
  157.9 11.4 %collective-permute-start.7 = (bf16[512,512]{0,1:T(8,128)(2,1)}, bf16[512,512]{0,1:T(8,128)(2,1)}, u32[]{:S(2)}, u32[]{:S(2)}) collective-permute-start(bf16[512,512]{0,1:T(8,128)(2,1)} %collective-permute-done.6), channel_id=1, source_target_pairs={{0,4},{4,8},{8,12},{12,16},{16,20},{20,24},{24,28},{28,32},{32,36}... | collective-permute-start | bytes 1572872 | tf_op jit(solution)/shard_map/ppermute | solution.py:112
  169.3 4.9 %compare_and_fusion = pred[512,8192]{1,0:T(8,128)(4,1)} fusion(s32[8192]{0:T(1024)S(1)} %add_select_fusion, s32[512]{0:T(512)S(1)} %add_select_fusion.1, pred[8192]{0:T(1024)(128)(4,1)S(1)} %broadcast_compare_fusion), kind=kLoop, calls=%fused_computation.7 | loop fusion | flops 8388608 | bytes 4237312 | tf_op jit(solution)/shard_map/and | solution.py:146
  174.3 4.8 collective-permute-start.14
  179.1 9.3 %collective-permute-done.7 = bf16[512,512]{0,1:T(8,128)(2,1)} collective-permute-done((bf16[512,512]{0,1:T(8,128)(2,1)}, bf16[512,512]{0,1:T(8,128)(2,1)}, u32[]{:S(2)}, u32[]{:S(2)}) %collective-permute-start.7) | collective-permute-done | bytes 524320 | tf_op jit(solution)/shard_map/ppermute | solution.py:112
  202.4 1.9 constant_dynamic-update-slice_fusion.23
  205.2 1.9 constant_dynamic-update-slice_fusion.21
  207.1 1.9 constant_dynamic-update-slice_fusion.20
  209.0 1.9 constant_dynamic-update-slice_fusion.19
  233.6 1.9 constant_dynamic-update-slice_fusion.1
  236.4 7.7 %constant_dynamic-slice_fusion = bf16[8192,512]{0,1:T(8,128)(2,1)} fusion(bf16[16384,512]{0,1:T(8,128)(2,1)} %constant_dynamic-update-slice_fusion, s32[]{:T(128)S(6)} %select_n.125), kind=kLoop, calls=%fused_computation.150 | loop fusion | bytes 16777220 | tf_op jit(solution)/shard_map/jit(_roll_dynamic)/dynamic_slice | solution.py:116
  244.1 29.0 %fusion = (f32[4,512]{1,0:T(4,128)S(1)}, f32[4,512,8192]{2,1,0:T(8,128)}) fusion(pred[512,8192]{1,0:T(8,128)(4,1)} %compare_and_fusion, bf16[512,4,128]{0,2,1:T(8,128)(2,1)} %bitcast.80, bf16[8192,4,128]{0,2,1:T(8,128)(2,1)} %bitcast.85), kind=kOutput, calls=%fused_computation.2 | convolution fusion | flops 4345296896 | bytes 80224256 | tf_op jit(solution)/shard_map/qhe,khe->hqk/dot_general | solution.py:143
  273.1 22.9 %fusion.1 = f32[4,512]{1,0:T(4,128)S(1)} fusion(f32[4,512,8192]{2,1,0:T(8,128)} %get-tuple-element.36, f32[4,512]{1,0:T(4,128)S(1)} %broadcast_maximum_fusion, pred[512,8192]{1,0:T(8,128)(4,1)} %compare_and_fusion), kind=kLoop, calls=%fused_computation.3 | loop fusion | flops 83884032 | bytes 71319552 | tf_op jit(solution)/shard_map/reduce_sum | solution.py:150
  296.0 29.0 %divide_convert_fusion = bf16[512,4,128]{0,2,1:T(8,128)(2,1)S(1)} fusion(bf16[8192,4,128]{0,2,1:T(8,128)(2,1)} %bitcast.75, f32[4,512,8192]{2,1,0:T(8,128)} %get-tuple-element.36, f32[4,512]{1,0:T(4,128)S(1)} %broadcast_maximum_fusion, pred[512,8192]{1,0:T(8,128)(4,1)} %compare_and_fusion, f32[512,4]{0,1:T(4,128)S(1)} %bitcast.84), kind=kOutput, calls=%fused_computation.46 | convolution fusion | flops 4379377664 | bytes 80232448 | tf_op jit(solution)/shard_map/hqk,khe->hqe/dot_general | solution.py:151
  326.3 26.7 %all_to_all.36 = bf16[4,128,2048]{2,1,0:T(8,128)(2,1)S(1)} all-to-all(bf16[4,128,2048]{2,1,0:T(8,128)(2,1)S(1)} %bitcast.78), channel_id=1, replica_groups=mesh['dp'=2,'seq'=16,'tensor'=4] {'tensor'}, dimensions={0} | all-to-all | bytes 4194304 | tf_op jit(solution)/shard_map/all_to_all | solution.py:34
  355.9 21.4 %all_to_all.37 = bf16[4,128,2048]{2,1,0:T(8,128)(2,1)} all-to-all(bf16[4,128,2048]{2,1,0:T(8,128)(2,1)S(1)} %broadcast_in_dim.108), channel_id=1, replica_groups=mesh['dp'=2,'seq'=16,'tensor'=4] {'tensor'}, dimensions={0} | all-to-all | bytes 4194304 | tf_op jit(solution)/shard_map/all_to_all | solution.py:19
  377.3 16.6 %convolution_convert_fusion = bf16[512,2048]{1,0:T(8,128)(2,1)} fusion(bf16[2048,2048]{1,0:T(8,128)(2,1)} %param.17, bf16[512,2048]{1,0:T(8,128)(2,1)} %bitcast.79, bf16[2048,2048]{1,0:T(8,128)(2,1)} %param.16), kind=kOutput, calls=%fused_computation.19 | convolution fusion | flops 8600420352 | bytes 20971520 | tf_op jit(solution)/shard_map/dot_general | solution.py:174
  393.9 4.4 all-to-all-start.3
  398.4 17.0 %all-to-all-done.3 = bf16[4,128,2048]{2,1,0:T(8,128)(2,1)} async-done(((bf16[4,128,2048]{2,1,0:T(8,128)(2,1)}), bf16[4,128,2048]{2,1,0:T(8,128)(2,1)}, u32[]{:S(2)}, u32[]{:S(2)}) %all-to-all-start.3) | async-done | bytes 2097184 | tf_op jit(solution)/shard_map/all_to_all | solution.py:34
  415.5 2.1 convert_reduce_fusion
  420.4 3.3 all-to-all-start.4
  424.4 3.8 all-to-all-done.4
  429.8 3.5 all-to-all-start.5
  435.8 5.0 %all-to-all-done.5 = f32[16,2,2048]{2,1,0:T(2,128)S(1)} async-done(((f32[16,2,2048]{2,1,0:T(2,128)}), f32[16,2,2048]{2,1,0:T(2,128)S(1)}, u32[]{:S(2)}, u32[]{:S(2)}) %all-to-all-start.5) | async-done | bytes 262176 | tf_op jit(solution)/shard_map/all_to_all | solution.py:19
  443.8 2.6 fusion.52
  446.4 2.0 pad_maximum_fusion.1
  449.7 16.1 %all-to-all-start.6 = ((f32[32,3,2]{1,2,0:T(2,128)}), f32[32,3,2]{1,2,0:T(2,128)S(1)}, u32[]{:S(2)}, u32[]{:S(2)}) async-start(f32[32,3,2]{1,2,0:T(2,128)} %broadcast_in_dim.118), calls=%async_computation.6 | async-start | bytes 65536 | tf_op jit(solution)/shard_map/all_to_all | solution.py:19
  465.8 2.3 fusion.34
  468.2 4.7 all-to-all-done.6
  475.7 3.1 multiply_select_fusion.2
  (140 shorter events, 63.4 us)
Async XLA Ops:
  7.2 317.8 %copy-start = (bf16[512,2048]{1,0:T(8,128)(2,1)S(1)}, bf16[512,2048]{1,0:T(8,128)(2,1)}, u32[]{:S(2)}) copy-start(bf16[512,2048]{1,0:T(8,128)(2,1)} %param.14) | copy-start | bytes 6291460
  7.2 236.9 %all-gather.3.cloned.1.call-start = ((), (), s32[]{:S(2)}) async-start(), calls=%async_computation.7 | async-start | bytes 8912896 | tf_op jit(solution)/shard_map/all_gather | solution.py:137
  41.2 90.5 %copy-start.21 = (s32[2]{0:T(128)S(1)}, s32[2]{0:T(128)}, u32[]{:S(2)}) copy-start(s32[2]{0:T(128)} %param.21) | copy-start | bytes 28
  47.5 1.2 copy-start.3
  49.8 15.4 %copy-start.16 = (bf16[512,512]{0,1:T(8,128)(2,1)}, bf16[512,512]{0,1:T(8,128)(2,1)S(1)}, u32[]{:S(2)}) copy-start(bf16[512,512]{0,1:T(8,128)(2,1)S(1)} %get-tuple-element.21) | copy-start | bytes 1572868
  49.8 15.4 %collective-permute-start = (bf16[512,512]{0,1:T(8,128)(2,1)S(1)}, bf16[512,512]{0,1:T(8,128)(2,1)S(1)}, u32[]{:S(2)}, u32[]{:S(2)}) collective-permute-start(bf16[512,512]{0,1:T(8,128)(2,1)S(1)} %get-tuple-element.21), channel_id=1, source_target_pairs={{0,4},{4,8},{8,12},{12,16},{16,20},{20,24},{24,28},{28,32},{32,36}... | collective-permute-start | bytes 1572872 | tf_op jit(solution)/shard_map/ppermute | solution.py:112
  65.2 18.4 %collective-permute-start.1 = (bf16[512,512]{0,1:T(8,128)(2,1)S(1)}, bf16[512,512]{0,1:T(8,128)(2,1)S(1)}, u32[]{:S(2)}, u32[]{:S(2)}) collective-permute-start(bf16[512,512]{0,1:T(8,128)(2,1)S(1)} %collective-permute-done), channel_id=1, source_target_pairs={{0,4},{4,8},{8,12},{12,16},{16,20},{20,24},{24,28},{28,32},{32,36}... | collective-permute-start | bytes 1572872 | tf_op jit(solution)/shard_map/ppermute | solution.py:112
  65.2 19.2 %collective-permute-start.8 = (bf16[512,512]{0,1:T(8,128)(2,1)}, bf16[512,512]{0,1:T(8,128)(2,1)S(1)}, u32[]{:S(2)}, u32[]{:S(2)}) collective-permute-start(bf16[512,512]{0,1:T(8,128)(2,1)} %copy-done.16), channel_id=1, source_target_pairs={{0,60},{4,0},{8,4},{12,8},{16,12},{20,16},{24,20},{28,24},{32,28},... | collective-permute-start | bytes 1572872 | tf_op jit(solution)/shard_map/ppermute | solution.py:114
  83.5 13.9 %copy-start.4 = (bf16[512,512]{0,1:T(8,128)(2,1)}, bf16[512,512]{0,1:T(8,128)(2,1)S(1)}, u32[]{:S(2)}) copy-start(bf16[512,512]{0,1:T(8,128)(2,1)S(1)} %collective-permute-done.1) | copy-start | bytes 1572868
  83.5 11.9 %collective-permute-start.2 = (bf16[512,512]{0,1:T(8,128)(2,1)S(1)}, bf16[512,512]{0,1:T(8,128)(2,1)S(1)}, u32[]{:S(2)}, u32[]{:S(2)}) collective-permute-start(bf16[512,512]{0,1:T(8,128)(2,1)S(1)} %collective-permute-done.1), channel_id=1, source_target_pairs={{0,4},{4,8},{8,12},{12,16},{16,20},{20,24},{24,28},{28,32},{32,36}... | collective-permute-start | bytes 1572872 | tf_op jit(solution)/shard_map/ppermute | solution.py:112
  84.4 13.0 %collective-permute-start.9 = (bf16[512,512]{0,1:T(8,128)(2,1)S(1)}, bf16[512,512]{0,1:T(8,128)(2,1)S(1)}, u32[]{:S(2)}, u32[]{:S(2)}) collective-permute-start(bf16[512,512]{0,1:T(8,128)(2,1)S(1)} %collective-permute-done.8), channel_id=1, source_target_pairs={{0,60},{4,0},{8,4},{12,8},{16,12},{20,16},{24,20},{28,24},{32,28},... | collective-permute-start | bytes 1572872 | tf_op jit(solution)/shard_map/ppermute | solution.py:114
  95.4 14.2 %copy-start.8 = (bf16[512,512]{0,1:T(8,128)(2,1)}, bf16[512,512]{0,1:T(8,128)(2,1)S(1)}, u32[]{:S(2)}) copy-start(bf16[512,512]{0,1:T(8,128)(2,1)S(1)} %collective-permute-done.2) | copy-start | bytes 1572868
  95.4 11.4 %collective-permute-start.3 = (bf16[512,512]{0,1:T(8,128)(2,1)S(1)}, bf16[512,512]{0,1:T(8,128)(2,1)S(1)}, u32[]{:S(2)}, u32[]{:S(2)}) collective-permute-start(bf16[512,512]{0,1:T(8,128)(2,1)S(1)} %collective-permute-done.2), channel_id=1, source_target_pairs={{0,4},{4,8},{8,12},{12,16},{16,20},{20,24},{24,28},{28,32},{32,36}... | collective-permute-start | bytes 1572872 | tf_op jit(solution)/shard_map/ppermute | solution.py:112
  97.4 5.5 %copy-start.6 = (bf16[512,512]{0,1:T(8,128)(2,1)}, bf16[512,512]{0,1:T(8,128)(2,1)S(1)}, u32[]{:S(2)}) copy-start(bf16[512,512]{0,1:T(8,128)(2,1)S(1)} %collective-permute-done.9) | copy-start | bytes 1572868
  97.4 12.2 %collective-permute-start.10 = (bf16[512,512]{0,1:T(8,128)(2,1)S(1)}, bf16[512,512]{0,1:T(8,128)(2,1)S(1)}, u32[]{:S(2)}, u32[]{:S(2)}) collective-permute-start(bf16[512,512]{0,1:T(8,128)(2,1)S(1)} %collective-permute-done.9), channel_id=1, source_target_pairs={{0,60},{4,0},{8,4},{12,8},{16,12},{20,16},{24,20},{28,24},{32,28},... | collective-permute-start | bytes 1572872 | tf_op jit(solution)/shard_map/ppermute | solution.py:114
  106.8 14.5 %copy-start.12 = (bf16[512,512]{0,1:T(8,128)(2,1)}, bf16[512,512]{0,1:T(8,128)(2,1)S(1)}, u32[]{:S(2)}) copy-start(bf16[512,512]{0,1:T(8,128)(2,1)S(1)} %collective-permute-done.3) | copy-start | bytes 1572868
  106.8 11.9 %collective-permute-start.4 = (bf16[512,512]{0,1:T(8,128)(2,1)S(1)}, bf16[512,512]{0,1:T(8,128)(2,1)S(1)}, u32[]{:S(2)}, u32[]{:S(2)}) collective-permute-start(bf16[512,512]{0,1:T(8,128)(2,1)S(1)} %collective-permute-done.3), channel_id=1, source_target_pairs={{0,4},{4,8},{8,12},{12,16},{16,20},{20,24},{24,28},{28,32},{32,36}... | collective-permute-start | bytes 1572872 | tf_op jit(solution)/shard_map/ppermute | solution.py:112
  109.6 5.5 %copy-start.10 = (bf16[512,512]{0,1:T(8,128)(2,1)}, bf16[512,512]{0,1:T(8,128)(2,1)S(1)}, u32[]{:S(2)}) copy-start(bf16[512,512]{0,1:T(8,128)(2,1)S(1)} %collective-permute-done.10) | copy-start | bytes 1572868
  109.6 11.6 %collective-permute-start.11 = (bf16[512,512]{0,1:T(8,128)(2,1)S(1)}, bf16[512,512]{0,1:T(8,128)(2,1)}, u32[]{:S(2)}, u32[]{:S(2)}) collective-permute-start(bf16[512,512]{0,1:T(8,128)(2,1)S(1)} %collective-permute-done.10), channel_id=1, source_target_pairs={{0,60},{4,0},{8,4},{12,8},{16,12},{20,16},{24,20},{28,24},{32,28},... | collective-permute-start | bytes 1572872 | tf_op jit(solution)/shard_map/ppermute | solution.py:114
  118.6 8.0 %copy-start.14 = (bf16[512,512]{0,1:T(8,128)(2,1)}, bf16[512,512]{0,1:T(8,128)(2,1)S(1)}, u32[]{:S(2)}) copy-start(bf16[512,512]{0,1:T(8,128)(2,1)S(1)} %collective-permute-done.4) | copy-start | bytes 1572868
  118.6 13.1 %collective-permute-start.5 = (bf16[512,512]{0,1:T(8,128)(2,1)S(1)}, bf16[512,512]{0,1:T(8,128)(2,1)}, u32[]{:S(2)}, u32[]{:S(2)}) collective-permute-start(bf16[512,512]{0,1:T(8,128)(2,1)S(1)} %collective-permute-done.4), channel_id=1, source_target_pairs={{0,4},{4,8},{8,12},{12,16},{16,20},{20,24},{24,28},{28,32},{32,36}... | collective-permute-start | bytes 1572872 | tf_op jit(solution)/shard_map/ppermute | solution.py:112
  121.3 18.3 %collective-permute-start.12 = (bf16[512,512]{0,1:T(8,128)(2,1)}, bf16[512,512]{0,1:T(8,128)(2,1)}, u32[]{:S(2)}, u32[]{:S(2)}) collective-permute-start(bf16[512,512]{0,1:T(8,128)(2,1)} %collective-permute-done.11), channel_id=1, source_target_pairs={{0,60},{4,0},{8,4},{12,8},{16,12},{20,16},{24,20},{28,24},{32,28},... | collective-permute-start | bytes 1572872 | tf_op jit(solution)/shard_map/ppermute | solution.py:114
  131.7 26.2 %collective-permute-start.6 = (bf16[512,512]{0,1:T(8,128)(2,1)}, bf16[512,512]{0,1:T(8,128)(2,1)}, u32[]{:S(2)}, u32[]{:S(2)}) collective-permute-start(bf16[512,512]{0,1:T(8,128)(2,1)} %collective-permute-done.5), channel_id=1, source_target_pairs={{0,4},{4,8},{8,12},{12,16},{16,20},{20,24},{24,28},{28,32},{32,36}... | collective-permute-start | bytes 1572872 | tf_op jit(solution)/shard_map/ppermute | solution.py:112
  139.6 34.7 %collective-permute-start.13 = (bf16[512,512]{0,1:T(8,128)(2,1)}, bf16[512,512]{0,1:T(8,128)(2,1)}, u32[]{:S(2)}, u32[]{:S(2)}) collective-permute-start(bf16[512,512]{0,1:T(8,128)(2,1)} %collective-permute-done.12), channel_id=1, source_target_pairs={{0,60},{4,0},{8,4},{12,8},{16,12},{20,16},{24,20},{28,24},{32,28},... | collective-permute-start | bytes 1572872 | tf_op jit(solution)/shard_map/ppermute | solution.py:114
  157.9 30.5 %collective-permute-start.7 = (bf16[512,512]{0,1:T(8,128)(2,1)}, bf16[512,512]{0,1:T(8,128)(2,1)}, u32[]{:S(2)}, u32[]{:S(2)}) collective-permute-start(bf16[512,512]{0,1:T(8,128)(2,1)} %collective-permute-done.6), channel_id=1, source_target_pairs={{0,4},{4,8},{8,12},{12,16},{16,20},{20,24},{24,28},{28,32},{32,36}... | collective-permute-start | bytes 1572872 | tf_op jit(solution)/shard_map/ppermute | solution.py:112
  174.2 46.9 %copy-start.15 = (bf16[512,512]{0,1:T(8,128)(2,1)S(1)}, bf16[512,512]{0,1:T(8,128)(2,1)}, u32[]{:S(2)}) copy-start(bf16[512,512]{0,1:T(8,128)(2,1)} %copy-done.14) | copy-start | bytes 1572868
  174.2 47.8 %copy-start.13 = (bf16[512,512]{0,1:T(8,128)(2,1)S(1)}, bf16[512,512]{0,1:T(8,128)(2,1)}, u32[]{:S(2)}) copy-start(bf16[512,512]{0,1:T(8,128)(2,1)} %copy-done.12) | copy-start | bytes 1572868
  174.2 48.6 %copy-start.9 = (bf16[512,512]{0,1:T(8,128)(2,1)S(1)}, bf16[512,512]{0,1:T(8,128)(2,1)}, u32[]{:S(2)}) copy-start(bf16[512,512]{0,1:T(8,128)(2,1)} %copy-done.8) | copy-start | bytes 1572868
  174.2 49.5 %copy-start.5 = (bf16[512,512]{0,1:T(8,128)(2,1)S(1)}, bf16[512,512]{0,1:T(8,128)(2,1)}, u32[]{:S(2)}) copy-start(bf16[512,512]{0,1:T(8,128)(2,1)} %copy-done.4) | copy-start | bytes 1572868
  174.2 53.9 %copy-start.7 = (bf16[512,512]{0,1:T(8,128)(2,1)S(1)}, bf16[512,512]{0,1:T(8,128)(2,1)}, u32[]{:S(2)}) copy-start(bf16[512,512]{0,1:T(8,128)(2,1)} %copy-done.6) | copy-start | bytes 1572868
  174.2 54.7 %copy-start.11 = (bf16[512,512]{0,1:T(8,128)(2,1)S(1)}, bf16[512,512]{0,1:T(8,128)(2,1)}, u32[]{:S(2)}) copy-start(bf16[512,512]{0,1:T(8,128)(2,1)} %copy-done.10) | copy-start | bytes 1572868
  174.3 40.4 %collective-permute-start.14 = (bf16[512,512]{0,1:T(8,128)(2,1)}, bf16[512,512]{0,1:T(8,128)(2,1)S(1)}, u32[]{:S(2)}, u32[]{:S(2)}) collective-permute-start(bf16[512,512]{0,1:T(8,128)(2,1)} %collective-permute-done.13), channel_id=1, source_target_pairs={{0,60},{4,0},{8,4},{12,8},{16,12},{20,16},{24,20},{28,24},{32,28},... | collective-permute-start | bytes 1572872 | tf_op jit(solution)/shard_map/ppermute | solution.py:114
  296.0 59.5 %copy-start.18 = (f32[2048]{0:T(1024)S(1)}, f32[2048]{0:T(1024)}, u32[]{:S(2)}) copy-start(f32[2048]{0:T(1024)} %param.15) | copy-start | bytes 24580
  354.7 0.8 copy-start.2
  377.3 21.1 %copy-start.19 = (f32[2048]{0:T(1024)S(1)}, f32[2048]{0:T(1024)}, u32[]{:S(2)}) copy-start(f32[2048]{0:T(1024)} %param.18) | copy-start | bytes 24580
  377.3 50.9 %copy-start.20 = (f32[2048]{0:T(1024)S(1)}, f32[2048]{0:T(1024)}, u32[]{:S(2)}) copy-start(f32[2048]{0:T(1024)} %param.19) | copy-start | bytes 24580
  377.3 56.0 %copy-start.22 = (s32[2]{0:T(128)S(1)}, s32[2]{0:T(128)}, u32[]{:S(2)}) copy-start(s32[2]{0:T(128)} %param.21) | copy-start | bytes 28
  393.9 21.5 %all-to-all-start.3 = ((bf16[4,128,2048]{2,1,0:T(8,128)(2,1)}), bf16[4,128,2048]{2,1,0:T(8,128)(2,1)}, u32[]{:S(2)}, u32[]{:S(2)}) async-start(bf16[4,128,2048]{2,1,0:T(8,128)(2,1)} %bitcast.76), calls=%async_computation.3 | async-start | bytes 4194304 | tf_op jit(solution)/shard_map/all_to_all | solution.py:34
  417.6 1.0 copy-start.1
  420.4 7.7 %all-to-all-start.4 = ((f32[4,2,2048]{2,1,0:T(2,128)}), f32[4,2,2048]{2,1,0:T(2,128)S(1)}, u32[]{:S(2)}, u32[]{:S(2)}) async-start(f32[4,2,2048]{2,1,0:T(2,128)} %broadcast_in_dim.110), calls=%async_computation.4 | async-start | bytes 131072 | tf_op jit(solution)/shard_map/all_to_all | solution.py:19
  428.3 1.5 copy-start.17
  429.8 11.0 %all-to-all-start.5 = ((f32[16,2,2048]{2,1,0:T(2,128)}), f32[16,2,2048]{2,1,0:T(2,128)S(1)}, u32[]{:S(2)}, u32[]{:S(2)}) async-start(f32[16,2,2048]{2,1,0:T(2,128)} %broadcast_in_dim.113), calls=%async_computation.5 | async-start | bytes 524288 | tf_op jit(solution)/shard_map/all_to_all | solution.py:19
  449.7 23.1 %all-to-all-start.6 = ((f32[32,3,2]{1,2,0:T(2,128)}), f32[32,3,2]{1,2,0:T(2,128)S(1)}, u32[]{:S(2)}, u32[]{:S(2)}) async-start(f32[32,3,2]{1,2,0:T(2,128)} %broadcast_in_dim.118), calls=%async_computation.6 | async-start | bytes 65536 | tf_op jit(solution)/shard_map/all_to_all | solution.py:19
Sparse Core Ops, SparseCore 0:
  49.9 140.6 all-gather.2
